TPU v7x, 32 devices: a whole 2x2x4 slice. The times are simulated.
32 devices in a mesh: row: 4 (over y, x), col: 8 (over z, core).
Axes of the slice: x: 2, y: 2, z: 4, core: 2. Of those that a mesh axis runs over, the one named last changes fastest.
Arguments:
- view_a: bfloat16 [3072, 8192], P(('row', 'col')), may hold values from -1000 to 1000
- view_b: bfloat16 [3072, 8192], P(('row', 'col')), may hold values from -1000 to 1000
Outputs:
- correlation: float32 [8192, 8192], P('row', 'col')
- loss: float32 [], replicated
All inputs are finite; a program needn't handle non-finite values.
Results may differ from a plain program's by a relative error of at most 0.0013.
Values may be sent and summed in bfloat16 or wider, within the bound.
A program may use at most 192 MiB of HBM per device.

v0:
```python
import jax
import jax.numpy as jnp
from jax import lax
from jax.sharding import PartitionSpec as P


def moments(view):
    values = view.astype(jnp.float32)
    return (jnp.sum(values, 0), jnp.sum(values * values, 0))


def scaled(view, total, squares, count):
    mean = total / count
    var = squares / count - mean * mean
    return ((view.astype(jnp.float32) - mean) * lax.rsqrt(var + 1e-05)).astype(jnp.bfloat16)


def shards(view_a, view_b):
    rows_local = view_a.shape[0]
    width = view_a.shape[1]
    n_row = lax.axis_size("row")
    n_col = lax.axis_size("col")
    count = rows_local * n_row * n_col
    left = lax.all_to_all(view_a, "row", split_axis=1, concat_axis=0, tiled=True)
    right = lax.all_to_all(view_b, "col", split_axis=1, concat_axis=0, tiled=True)
    part_total, part_squares = moments(left)
    part_total, part_squares = lax.psum((part_total, part_squares), "col")
    left = scaled(left, part_total, part_squares, count)
    side_total, side_squares = moments(right)
    side_total, side_squares = lax.psum((side_total, side_squares), "row")
    right = scaled(right, side_total, side_squares, count)
    row_block = left.shape[1]
    col_block = right.shape[1]
    every_left = lax.all_gather(left, "col", axis=0, tiled=True)
    grouped = every_left.reshape(n_col, n_row, rows_local, row_block)
    piece = lax.all_gather(right, "row", axis=0, tiled=True)
    groups = piece.shape[0] // right.shape[0]
    blocks = piece.reshape(groups, n_col, rows_local, col_block)
    product = jnp.einsum("ckbf,kcbg->fg", grouped, blocks, preferred_element_type=jnp.float32)
    correlation = product / count
    row_ids = lax.axis_index("row") * row_block + lax.broadcasted_iota(jnp.int32, (row_block, 1), 0)
    col_ids = lax.axis_index("col") * col_block + lax.broadcasted_iota(jnp.int32, (1, col_block), 1)
    on_diag = row_ids == col_ids
    squared = correlation * correlation
    diag_terms = jnp.where(on_diag, (1.0 - correlation) ** 2 - 0.0051 * squared, 0.0)
    partial_loss = 0.0051 * jnp.sum(squared) + jnp.sum(diag_terms)
    loss = lax.psum(partial_loss, ("row", "col")) / width
    return (correlation, loss)


def solution(mesh):
    return jax.shard_map(
        shards,
        mesh=mesh,
        in_specs=(P(("row", "col"), None), P(("row", "col"), None)),
        out_specs=(P("row", "col"), P()),
        check_vma=False,
    )
```

profile of v0, /device:TPU:12, one launch (start us, length us, event | category | flops | bytes accessed | tf_op | source)
XLA Modules:
  0.0 330.5 jit_solution(2563064573535867003)
XLA Ops:
  7.2 0.0 all-gather.5.cloned.1.call-start
  7.2 1.5 copy.26
  8.8 40.6 %all_to_all.26 = bf16[96,8,1024]{2,0,1:T(8,128)(2,1)S(1)} all-to-all(bf16[96,8,1024]{2,0,1:T(8,128)(2,1)S(1)} %bitcast.31), channel_id=1, replica_groups=mesh['row'=4,'col'=8] {'col'}, dimensions={1} | all-to-all | bytes 3145728 | tf_op jit(solution)/shard_map/all_to_all | solution.py:25
  49.4 0.0 copy-start
  49.4 0.5 convert_reduce_fusion
  49.8 9.1 %all-reduce.1 = (f32[1024]{0:T(1024)S(1)}, f32[1024]{0:T(1024)S(1)}) all-reduce(f32[1024]{0:T(1024)S(1)} %get-tuple-element.5, f32[1024]{0:T(1024)S(1)} %get-tuple-element.4), channel_id=1, replica_groups=mesh['row'=4,'col'=8] {'row'}, use_global_device_ids=true, to_apply=%region_7.0 | all-reduce | flops 2048 | bytes 16384 | tf_op jit(solution)/shard_map/psum | solution.py:30
  59.0 1.6 fusion.5
  60.6 0.0 all-gather.5.cloned.1.call-update
  60.6 0.0 all-gather.3.cloned.1.call-start
  60.7 0.0 copy-done
  60.7 0.2 copy.27
  60.8 33.6 %all_to_all.27 = bf16[96,4,2048]{2,0,1:T(8,128)(2,1)S(1)} all-to-all(bf16[96,4,2048]{2,0,1:T(8,128)(2,1)S(1)} %bitcast.32), channel_id=1, replica_groups=mesh['row'=4,'col'=8] {'row'}, dimensions={1} | all-to-all | bytes 3145728 | tf_op jit(solution)/shard_map/all_to_all | solution.py:24
  94.4 0.4 convert_reduce_fusion.1
  94.9 26.0 %all-reduce = (f32[2048]{0:T(1024)S(1)}, f32[2048]{0:T(1024)S(1)}) all-reduce(f32[2048]{0:T(1024)S(1)} %get-tuple-element.7, f32[2048]{0:T(1024)S(1)} %get-tuple-element.6), channel_id=1, replica_groups=mesh['row'=4,'col'=8] {'col'}, use_global_device_ids=true, to_apply=%region_3.0 | all-reduce | flops 4096 | bytes 32768 | tf_op jit(solution)/shard_map/psum | solution.py:27
  120.9 1.6 fusion.7
  122.4 0.0 all-gather.3.cloned.1.call-update
  122.5 17.6 %all-gather.5.cloned.1.call-done = bf16[3072,1024]{1,0:T(8,128)(2,1)} async-done(((bf16[768,1024]{1,0:T(8,128)(2,1)}), bf16[3072,1024]{1,0:T(8,128)(2,1)}) %all-gather.5.cloned.1.call-update) | async-done | bytes 6291472 | tf_op jit(solution)/shard_map/all_gather | solution.py:36
  140.1 116.2 %all-gather.3.cloned.1.call-done = bf16[3072,2048]{1,0:T(8,128)(2,1)} async-done(((bf16[384,2048]{1,0:T(8,128)(2,1)}), bf16[3072,2048]{1,0:T(8,128)(2,1)}) %all-gather.3.cloned.1.call-update) | async-done | bytes 12582928 | tf_op jit(solution)/shard_map/all_gather | solution.py:34
  256.3 21.4 %select_reduce_fusion = (f32[]{:T(128)}, f32[]{:T(128)}, f32[2048,1024]{1,0:T(8,128)}) fusion(s32[1024]{0:T(1024)S(1)} %iota_add_fusion.1, s32[2048]{0:T(1024)S(1)} %iota_add_fusion, bf16[8,4,96,2048]{3,2,1,0:T(8,128)(2,1)} %bitcast.35, bf16[4,8,96,1024]{3,2,1,0:T(8,128)(2,1)} %bitcast.36), kind=kOutput, calls=%fused_computation.1 | convolution fusion | flops 12905873408 | bytes 27275272 | tf_op jit(solution)/shard_map/ckbf,kcbg->fg/dot_general | solution.py:39
  279.0 43.0 %psum.39 = f32[]{:T(128)} all-reduce(f32[]{:T(128)S(6)} %add.55), channel_id=1, replica_groups=mesh['row'=4,'col'=8] {'row','col'}, use_global_device_ids=true, to_apply=%region_10.11 | all-reduce | flops 1 | bytes 8 | tf_op jit(solution)/shard_map/psum | solution.py:47
  (4 shorter events, 0.0 us)
Async XLA Ops:
  7.2 132.9 %all-gather.5.cloned.1.call-start = ((), (), s32[]{:S(2)}) async-start(), calls=%async_computation.3 | async-start | bytes 7864320 | tf_op jit(solution)/shard_map/all_gather | solution.py:36
  49.4 11.3 %copy-start = (bf16[96,8192]{1,0:T(8,128)(2,1)S(1)}, bf16[96,8192]{1,0:T(8,128)(2,1)}, u32[]{:S(2)}) copy-start(bf16[96,8192]{1,0:T(8,128)(2,1)} %param.2) | copy-start | bytes 4718596
  60.6 195.7 %all-gather.3.cloned.1.call-start = ((), (), s32[]{:S(2)}) async-start(), calls=%async_computation.2 | async-start | bytes 14155776 | tf_op jit(solution)/shard_map/all_gather | solution.py:34
Sparse Core Ops, SparseCore 0:
  60.7 79.2 all-gather.4
  142.3 113.9 all-gather.2
where the time goes:
time: 331 us
  blocking collectives  152 us (46%)
  waiting for transfers between devices  134 us (40%)
  matrix products  21.4 us (6%)
  between operations  17.1 us (5%)
  other arithmetic  4.09 us (1%)
    all_gather x1, waiting for transfers between devices, shards(): every_left = lax.all_gather(left, 'col', axis=0, tiled=True)  116 us
    psum x1, blocking collectives, shards(): loss = lax.psum(partial_loss, ('row', 'col')) / width  43 us
    all_to_all x1, blocking collectives, shards(): lax.all_to_all(view_b, 'col', split_axis=1, concat_axis=0, tiled=True)  40.6 us
    all_to_all x1, blocking collectives, shards(): lax.all_to_all(view_a, 'row', split_axis=1, concat_axis=0, tiled=True)  33.6 us
    psum x1, blocking collectives, shards(): part_total, part_squares = lax.psum((part_total, part_squares), 'col')  26 us
    dot_general x1, matrix products, shards(): jnp.einsum('ckbf,kcbg->fg', grouped, blocks, preferred_element_type=jnp.f...  21.4 us
    all_gather x1, waiting for transfers between devices, shards(): piece = lax.all_gather(right, 'row', axis=0, tiled=True)  17.6 us
    psum x1, blocking collectives, shards(): side_total, side_squares = lax.psum((side_total, side_squares), 'row')  9.11 us
  transfers between devices with their start and end apart: 2, of which 2 were waited for; matrix products, arithmetic and copies ran while one was open for 1% of the time, Pallas kernels for 0%

commit v1 on v0

--- a/solution.py
+++ b/solution.py
@@ -21,7 +21,10 @@
     n_row = lax.axis_size("row")
     n_col = lax.axis_size("col")
     count = rows_local * n_row * n_col
-    left = lax.all_to_all(view_a, "row", split_axis=1, concat_axis=0, tiled=True)
+    left = jnp.concatenate(
+        lax.all_to_all(jnp.stack(jnp.split(view_a, lax.axis_size("row"), axis=1)), "row", 0, 0),
+        axis=0,
+    )
     right = lax.all_to_all(view_b, "col", split_axis=1, concat_axis=0, tiled=True)
     part_total, part_squares = moments(left)
     part_total, part_squares = lax.psum((part_total, part_squares), "col")

time: 331 us -> 331 us (level)
  no operation moved by 1% of the time
where the time goes in v1:
time: 331 us
  blocking collectives  152 us (46%)
  waiting for transfers between devices  134 us (40%)
  matrix products  21.4 us (6%)
  between operations  17.2 us (5%)
  other arithmetic  4.33 us (1%)
    all_gather x1, waiting for transfers between devices, shards(): every_left = lax.all_gather(left, 'col', axis=0, tiled=True)  116 us
    psum x1, blocking collectives, shards(): loss = lax.psum(partial_loss, ('row', 'col')) / width  43 us
    all_to_all x1, blocking collectives, shards(): lax.all_to_all(view_b, 'col', split_axis=1, concat_axis=0, tiled=True)  40.6 us
    all_to_all x1, blocking collectives, shards(): lax.all_to_all(jnp.stack(jnp.split(view_a, lax.axis_size('row'), axis=1))...  33.7 us
    psum x1, blocking collectives, shards(): part_total, part_squares = lax.psum((part_total, part_squares), 'col')  26 us
    dot_general x1, matrix products, shards(): jnp.einsum('ckbf,kcbg->fg', grouped, blocks, preferred_element_type=jnp.f...  21.4 us
    all_gather x1, waiting for transfers between devices, shards(): piece = lax.all_gather(right, 'row', axis=0, tiled=True)  17.4 us
    psum x1, blocking collectives, shards(): side_total, side_squares = lax.psum((side_total, side_squares), 'row')  9.11 us
  transfers between devices with their start and end apart: 2, of which 2 were waited for; matrix products, arithmetic and copies ran while one was open for 1% of the time, Pallas kernels for 0%

profile of v1, /device:TPU:12, one launch (start us, length us, event | category | flops | bytes accessed | tf_op | source)
XLA Modules:
  0.0 330.7 jit_solution(7954161227893274463)
XLA Ops:
  7.2 0.0 all-gather.5.cloned.1.call-start
  7.2 1.6 copy.18
  8.8 40.6 %all_to_all.18 = bf16[96,8,1024]{2,0,1:T(8,128)(2,1)S(1)} all-to-all(bf16[96,8,1024]{2,0,1:T(8,128)(2,1)S(1)} %bitcast.33), channel_id=1, replica_groups=mesh['row'=4,'col'=8] {'col'}, dimensions={1} | all-to-all | bytes 3145728 | tf_op jit(solution)/shard_map/all_to_all | solution.py:28
  49.4 0.0 copy-start
  49.4 0.5 convert_reduce_fusion
  49.9 9.1 %all-reduce.1 = (f32[1024]{0:T(1024)S(1)}, f32[1024]{0:T(1024)S(1)}) all-reduce(f32[1024]{0:T(1024)S(1)} %get-tuple-element.5, f32[1024]{0:T(1024)S(1)} %get-tuple-element.4), channel_id=1, replica_groups=mesh['row'=4,'col'=8] {'row'}, use_global_device_ids=true, to_apply=%region_7.0 | all-reduce | flops 2048 | bytes 16384 | tf_op jit(solution)/shard_map/psum | solution.py:33
  59.0 1.6 fusion.5
  60.6 0.0 all-gather.5.cloned.1.call-update
  60.6 0.0 all-gather.3.cloned.1.call-start
  60.7 0.0 copy-done
  60.7 0.1 slice_bitcast_fusion.3
  60.8 0.2 pad_maximum_fusion
  61.0 33.7 %all_to_all.19 = bf16[4,96,2048]{2,1,0:T(8,128)(2,1)S(1)} all-to-all(bf16[4,96,2048]{2,1,0:T(8,128)(2,1)S(1)} %pad_maximum_fusion), channel_id=1, replica_groups=mesh['row'=4,'col'=8] {'row'}, dimensions={0} | all-to-all | bytes 3145728 | tf_op jit(solution)/shard_map/all_to_all | solution.py:25
  94.7 0.4 convert_reduce_fusion.1
  95.2 26.0 %all-reduce = (f32[2048]{0:T(1024)S(1)}, f32[2048]{0:T(1024)S(1)}) all-reduce(f32[2048]{0:T(1024)S(1)} %get-tuple-element.7, f32[2048]{0:T(1024)S(1)} %get-tuple-element.6), channel_id=1, replica_groups=mesh['row'=4,'col'=8] {'col'}, use_global_device_ids=true, to_apply=%region_3.0 | all-reduce | flops 4096 | bytes 32768 | tf_op jit(solution)/shard_map/psum | solution.py:30
  121.2 1.6 fusion.7
  122.8 0.0 all-gather.3.cloned.1.call-update
  122.8 17.4 %all-gather.5.cloned.1.call-done = bf16[3072,1024]{1,0:T(8,128)(2,1)} async-done(((bf16[768,1024]{1,0:T(8,128)(2,1)}), bf16[3072,1024]{1,0:T(8,128)(2,1)}) %all-gather.5.cloned.1.call-update) | async-done | bytes 6291472 | tf_op jit(solution)/shard_map/all_gather | solution.py:39
  140.2 116.2 %all-gather.3.cloned.1.call-done = bf16[3072,2048]{1,0:T(8,128)(2,1)} async-done(((bf16[384,2048]{1,0:T(8,128)(2,1)}), bf16[3072,2048]{1,0:T(8,128)(2,1)}) %all-gather.3.cloned.1.call-update) | async-done | bytes 12582928 | tf_op jit(solution)/shard_map/all_gather | solution.py:37
  256.4 21.4 %select_reduce_fusion = (f32[]{:T(128)}, f32[]{:T(128)}, f32[2048,1024]{1,0:T(8,128)}) fusion(s32[1024]{0:T(1024)S(1)} %iota_add_fusion.1, s32[2048]{0:T(1024)S(1)} %iota_add_fusion, bf16[8,4,96,2048]{3,2,1,0:T(8,128)(2,1)} %bitcast.35, bf16[4,8,96,1024]{3,2,1,0:T(8,128)(2,1)} %bitcast.36), kind=kOutput, calls=%fused_computation.1 | convolution fusion | flops 12905873408 | bytes 27275272 | tf_op jit(solution)/shard_map/ckbf,kcbg->fg/dot_general | solution.py:42
  279.1 43.0 %psum.39 = f32[]{:T(128)} all-reduce(f32[]{:T(128)S(6)} %add.55), channel_id=1, replica_groups=mesh['row'=4,'col'=8] {'row','col'}, use_global_device_ids=true, to_apply=%region_10.11 | all-reduce | flops 1 | bytes 8 | tf_op jit(solution)/shard_map/psum | solution.py:50
  (4 shorter events, 0.0 us)
Async XLA Ops:
  7.2 133.1 %all-gather.5.cloned.1.call-start = ((), (), s32[]{:S(2)}) async-start(), calls=%async_computation.3 | async-start | bytes 7864320 | tf_op jit(solution)/shard_map/all_gather | solution.py:39
  49.4 11.3 %copy-start = (bf16[96,8192]{1,0:T(8,128)(2,1)S(1)}, bf16[96,8192]{1,0:T(8,128)(2,1)}, u32[]{:S(2)}) copy-start(bf16[96,8192]{1,0:T(8,128)(2,1)} %param.2) | copy-start | bytes 4718596
  60.6 195.8 %all-gather.3.cloned.1.call-start = ((), (), s32[]{:S(2)}) async-start(), calls=%async_computation.2 | async-start | bytes 14155776 | tf_op jit(solution)/shard_map/all_gather | solution.py:37
Sparse Core Ops, SparseCore 0:
  60.7 79.4 all-gather.4
  142.4 113.9 all-gather.2
